TPU v7x, 32 devices: a whole 2x2x4 slice. The times are simulated.
32 devices in a mesh: date: 16 (over z, y, x), pix: 2 (over core).
Axes of the slice: x: 2, y: 2, z: 4, core: 2. Of those that a mesh axis runs over, the one named last changes fastest.
Arguments:
- reflect: bfloat16 [64, 6, 16384], P('date', None, 'pix'), may hold values from -8 to 8
- cloud_free: int32 [64, 16384], P('date', 'pix'), may hold values from 0 to 1, as said below
- days: int32 [64], P('date'), may hold values from 1 to 2079, as said below
Outputs:
- median: float32 [6, 16384], P(None, 'pix')
- slope: float32 [6, 16384], P(None, 'pix')
Inputs may be any that keep to these rules, and one draw needn't show every extreme that they name: `cloud_free`: every pixel is clear on at least one of the first 32 dates and on at least one of the others; clear shares differ between tiles. `days`: strictly increasing.
All inputs are finite; a program needn't handle non-finite values.
Results may differ from a plain program's by a relative error of at most 0.0003.
Values may be sent and summed in bfloat16 or wider, within the bound.
A program may use at most 64 MiB of HBM per device.

v0:
```python
import functools

import jax
import jax.numpy as jnp
from jax import lax
from jax.experimental import pallas as pl
from jax.experimental.pallas import tpu as pltpu
from jax.sharding import PartitionSpec as P

MESH = pl.DeviceIdType.MESH
ridge = 1.0
sentinel = 100.0
lanes = 128
slot = 8


def merge_pairs(lo, hi, r):
    step = r * 2
    if step < hi - lo:
        yield from merge_pairs(lo, hi, step)
        yield from merge_pairs(lo + r, hi, step)
        yield from ((i, i + r) for i in range(lo + r, hi - r, step))
    else:
        yield (lo, lo + r)


def sort_pairs(lo, hi):
    if hi - lo >= 1:
        mid = lo + (hi - lo) // 2
        yield from sort_pairs(lo, mid)
        yield from sort_pairs(mid + 1, hi)
        yield from merge_pairs(lo, hi, 1)


def sort_network(values):
    values = list(values)
    for i, j in sort_pairs(0, len(values) - 1):
        a, b = values[i], values[j]
        values[i], values[j] = jnp.minimum(a, b), jnp.maximum(a, b)
    return values


def kernel(
    n,
    pixes,
    group,
    x_hbm,
    m_hbm,
    days_ref,
    out_ref,
    x_ref,
    m_ref,
    wide,
    sent,
    got,
    part,
    parts,
    mean_row,
    mean_rows,
    stack,
    mean_tile,
    year_tile,
    flip,
    odd,
    load_sem,
    data_send,
    data_recv,
    part_send,
    part_recv,
    mean_send,
    mean_recv,
    far_send,
    far_recv,
    near_send,
    near_recv,
):
    me = lax.axis_index("date")
    pix = lax.axis_index("pix")
    bands, dates, tile = x_ref.shape
    width = tile // n
    total = n * dates
    lines = n // group
    line = me // group
    spot = lax.rem(me, group)
    pieces = sent.shape[0]
    span = width // pieces

    barrier = pltpu.get_barrier_semaphore()

    @pl.loop(1, n)
    def _(r):
        pl.semaphore_signal(barrier, inc=1, device_id={"date": lax.rem(me + r, n)}, device_id_type=MESH)

    for r in range(1, pixes):
        pl.semaphore_signal(barrier, inc=1, device_id={"pix": lax.rem(pix + r, pixes)}, device_id_type=MESH)

    load_x = pltpu.make_async_copy(x_hbm, x_ref, load_sem.at[0])
    load_m = pltpu.make_async_copy(m_hbm, m_ref, load_sem.at[1])
    load_x.start()
    load_m.start()
    stack[...] = jnp.zeros_like(stack)
    load_m.wait()
    load_x.wait()

    def mark(j, carry):
        cols = pl.ds(pl.multiple_of(j * width, lanes), width)
        valid = m_ref[:, cols] > 0
        out = []
        for b in range(bands):
            x = x_ref[b, :, cols].astype(jnp.float32)
            marked = jnp.where(valid, x, sentinel)
            for d in range(dates):
                wide[d * bands + b : d * bands + b + 1, :] = marked[d : d + 1, :]
            out.append(carry[b] + jnp.where(valid, x, 0.0))
        for p in range(pieces):
            sent[p, j] = wide[:, p * span : (p + 1) * span].astype(jnp.bfloat16)
        out.append(carry[bands] + jnp.where(valid, 1.0, 0.0))
        return tuple(out)

    zero = jnp.zeros((dates, width), jnp.float32)
    sums = lax.fori_loop(0, n, mark, tuple(zero for _ in range(bands + 1)))
    for p in range(pieces):
        got[p, me] = sent[p, me]

    lane = lax.broadcasted_iota(jnp.int32, (dates, lanes), 1)
    date = lax.broadcasted_iota(jnp.int32, (dates, lanes), 0)
    lane_row = lax.broadcasted_iota(jnp.int32, (1, lanes), 1)
    row = jnp.zeros((dates, lanes), jnp.float32)
    for b in range(bands):
        row = row + jnp.where(lane == date * slot + b, jnp.sum(sums[b], axis=1, keepdims=True), 0.0)
    own = (lane >= date * slot) & (lane < (date + 1) * slot)
    count_row = jnp.where(own, jnp.sum(sums[bands], axis=1, keepdims=True), 0.0)
    part[0:1, :] = jnp.sum(row, axis=0, keepdims=True)
    part[1:2, :] = jnp.sum(count_row, axis=0, keepdims=True)

    pl.semaphore_wait(barrier, n - 1 + pixes - 1)

    def part_copy(r):
        return pltpu.make_async_remote_copy(
            src_ref=part,
            dst_ref=parts.at[r],
            send_sem=part_send.at[r],
            recv_sem=part_recv.at[r],
            device_id={"pix": lax.rem(pix + r, pixes)},
            device_id_type=MESH,
        )

    for r in range(1, pixes):
        part_copy(r).start()

    def data_copy(p, r):
        j = lax.rem(me + r, n)
        return pltpu.make_async_remote_copy(
            src_ref=sent.at[p, j],
            dst_ref=got.at[p, me],
            send_sem=data_send.at[p, r],
            recv_sem=data_recv.at[p, r],
            device_id={"date": j},
            device_id_type=MESH,
        )

    def mean_copy(r):
        return pltpu.make_async_remote_copy(
            src_ref=mean_row,
            dst_ref=mean_rows.at[me],
            send_sem=mean_send.at[r],
            recv_sem=mean_recv.at[r],
            device_id={"date": lax.rem(me + r, n)},
            device_id_type=MESH,
        )

    @pl.loop(1, n)
    def _(r):
        data_copy(0, r).start()

    csum_row = part[0:1, :]
    cnt_row = part[1:2, :]
    for r in range(1, pixes):
        part_copy(r).wait_recv()
        csum_row = csum_row + parts[r, 0:1, :]
        cnt_row = cnt_row + parts[r, 1:2, :]
    means = csum_row / jnp.maximum(cnt_row, 1.0)
    years = jnp.zeros((1, lanes), jnp.float32)
    for d in range(dates):
        year = jnp.full((1, lanes), days_ref[d], jnp.int32).astype(jnp.float32) / 365.0
        years = jnp.where((lane_row >= d * slot) & (lane_row < (d + 1) * slot), year, years)
    mean_row[0:1, :] = means
    mean_row[1:2, :] = years
    mean_rows[me] = mean_row[...]

    @pl.loop(1, n)
    def _(r):
        mean_copy(r).start()

    for p in range(1, pieces):

        @pl.loop(1, n)
        def _(r):
            data_copy(p, r).start()

    @pl.loop(1, n)
    def _(r):
        mean_copy(r).wait_recv()

    for row_index, tile_ref in ((0, mean_tile), (1, year_tile)):
        for j in range(n):
            stack[j : j + 1, :] = mean_rows[j, row_index : row_index + 1, :]
        turned = jnp.transpose(stack[...])
        for j in range(n):
            for d in range(dates):
                column = turned[d * slot : d * slot + bands, j : j + 1]
                tile_ref[j * dates + d] = jnp.broadcast_to(column, (bands, lanes))

    def trend(p, r, carry):
        j = lax.rem(me + n - r, n)
        fill, s_zero, s_one, s_two, s_y, s_ty = carry
        block = got[p, j].astype(jnp.float32)
        for d in range(dates):
            x = block[d * bands : (d + 1) * bands, :]
            year = jnp.concatenate([year_tile[j * dates + d]] * (span // lanes), axis=1)
            mean = jnp.concatenate([mean_tile[j * dates + d]] * (span // lanes), axis=1)
            valid = x < 50.0
            y = jnp.where(valid, x - mean, 0.0)
            m = jnp.where(valid, 1.0, 0.0)
            tm = year * m
            s_zero = s_zero + m
            s_one = s_one + tm
            s_two = s_two + year * tm
            s_y = s_y + y
            s_ty = s_ty + year * y
            flip[r * dates + d] = jnp.where(valid, x, fill)
            fill = jnp.where(valid, fill, -fill)
        return (fill, s_zero, s_one, s_two, s_y, s_ty)

    def rank(p):
        blank = jnp.zeros((bands, span), jnp.float32)
        start = trend(p, 0, (blank + sentinel, blank, blank, blank, blank, blank))

        def arrived(r, carry):
            data_copy(p, r).wait_recv()
            return trend(p, r, carry)

        fill, s_zero, s_one, s_two, s_y, s_ty = lax.fori_loop(1, n, arrived, start)
        first = s_zero + ridge
        here = pl.ds(pl.multiple_of(me * width + p * span, lanes), span)
        out_ref[1, :, here] = (first * s_ty - s_one * s_y) / (first * (s_two + ridge) - s_one * s_one)
        odd[...] = jnp.where(fill < 0.0, 1.0, 0.0)

        @pl.loop(0, span // lanes)
        def _(k):
            cols = pl.ds(pl.multiple_of(k * lanes, lanes), lanes)
            half = total // 2
            low = sort_network([flip[i, :, cols] for i in range(half)])
            high = sort_network([flip[half + i, :, cols] for i in range(half)])
            lower = None
            upper = None
            for i in range(half):
                a, b = low[i], high[half - 1 - i]
                small, large = jnp.minimum(a, b), jnp.maximum(a, b)
                lower = small if lower is None else jnp.maximum(lower, small)
                upper = large if upper is None else jnp.minimum(upper, large)
            median = jnp.where(odd[:, cols] > 0.5, lower, 0.5 * (lower + upper))
            there = pl.ds(pl.multiple_of(me * width + p * span + k * lanes, lanes), lanes)
            out_ref[0, :, there] = median

    def out_copy(owner, p, target, send, recv):
        cols = pl.ds(pl.multiple_of(owner * width + p * span, lanes), span)
        return pltpu.make_async_remote_copy(
            src_ref=out_ref.at[:, :, cols],
            dst_ref=out_ref.at[:, :, cols],
            send_sem=send,
            recv_sem=recv,
            device_id={"date": target},
            device_id_type=MESH,
        )

    def partner(r):
        other = line
        for bit in range(lines.bit_length() - 1):
            if (r >> bit) & 1:
                other = other + (1 << bit) - (1 << (bit + 1)) * lax.rem(line // (1 << bit), 2)
        return other

    def far_copy(p, r):
        target = partner(r) * group + spot
        return out_copy(me, p, target, far_send.at[p, r], far_recv.at[p, r])

    def near_copy(p, r, s):
        owner = partner(r) * group + spot
        target = line * group + lax.rem(spot + s, group)
        return out_copy(owner, p, target, near_send.at[p, r, s], near_recv.at[p, r, s])

    for p in range(pieces):
        rank(p)

        for r in range(lines - 1, 0, -1):
            far_copy(p, r).start()
        for s in range(1, group):
            near_copy(p, 0, s).start()

    for p in range(pieces):
        for r in range(1, lines):
            far_copy(p, r).wait_recv()
            for s in range(1, group):
                near_copy(p, r, s).start()

    for r in range(1, pixes):
        part_copy(r).wait_send()

    @pl.loop(1, n)
    def _(r):
        mean_copy(r).wait_send()
        for p in range(pieces):
            data_copy(p, r).wait_send()

    for p in range(pieces):
        for r in range(1, lines):
            far_copy(p, r).wait_send()
        for r in range(lines):
            for s in range(1, group):
                near_copy(p, r, s).wait()


def local(n, pixes, reflect, cloud_free, days):
    dates, bands, tile = reflect.shape
    width = tile // n
    group = 1
    while group * group * 4 <= n and n % (group * 2) == 0:
        group *= 2
    pieces = 2 if width % (2 * lanes) == 0 else 1
    span = width // pieces
    lines = n // group
    turned = -(-n // lanes) * lanes
    vmem = pl.BlockSpec(memory_space=pltpu.VMEM)
    hbm = pl.BlockSpec(memory_space=pl.ANY)
    dma = pltpu.SemaphoreType.DMA
    out = pl.pallas_call(
        functools.partial(kernel, n, pixes, group),
        out_shape=pltpu.VMEM((2, bands, tile), jnp.float32),
        in_specs=[hbm, hbm, pl.BlockSpec(memory_space=pltpu.SMEM)],
        out_specs=vmem,
        scratch_shapes=[
            pltpu.VMEM((bands, dates, tile), jnp.bfloat16),
            pltpu.VMEM((dates, tile), jnp.int32),
            pltpu.VMEM((dates * bands, width), jnp.float32),
            pltpu.VMEM((pieces, n, dates * bands, span), jnp.bfloat16),
            pltpu.VMEM((pieces, n, dates * bands, span), jnp.bfloat16),
            pltpu.VMEM((2, lanes), jnp.float32),
            pltpu.VMEM((pixes, 2, lanes), jnp.float32),
            pltpu.VMEM((2, lanes), jnp.float32),
            pltpu.VMEM((n, 2, lanes), jnp.float32),
            pltpu.VMEM((turned, lanes), jnp.float32),
            pltpu.VMEM((n * dates, bands, lanes), jnp.float32),
            pltpu.VMEM((n * dates, bands, lanes), jnp.float32),
            pltpu.VMEM((n * dates, bands, span), jnp.float32),
            pltpu.VMEM((bands, span), jnp.float32),
            dma((2,)),
            dma((pieces, n)),
            dma((pieces, n)),
            dma((pixes,)),
            dma((pixes,)),
            dma((n,)),
            dma((n,)),
            dma((pieces, lines)),
            dma((pieces, lines)),
            dma((pieces, lines, group)),
            dma((pieces, lines, group)),
        ],
        compiler_params=pltpu.CompilerParams(collective_id=0, has_side_effects=True),
    )(jnp.transpose(reflect, (1, 0, 2)), cloud_free, days)
    return (out[0], out[1])


def solution(mesh):
    placed = (P("date", None, "pix"), P("date", "pix"), P("date"))
    return jax.shard_map(
        functools.partial(local, mesh.shape["date"], mesh.shape["pix"]),
        mesh=mesh,
        in_specs=placed,
        out_specs=(P(None, "pix"), P(None, "pix")),
        check_vma=False,
    )
```

profile of v0, /device:TPU:0, one launch (start us, length us, event | category | flops | bytes accessed | tf_op | source)
XLA Modules:
  0.0 29.6 jit_solution(14943659009709617152)
XLA Ops:
  0.6 28.2 %shard_map.50 = f32[2,6,8192]{2,1,0:T(8,128)S(1)} custom-call(bf16[6,4,8192]{2,1,0:T(4,128)(2,1)} %bitcast.5, s32[4,8192]{1,0:T(4,128)} %m_hbm.1, s32[4]{0:T(128)} %days_ref.1), custom_call_target="tpu_custom_call" | custom-call | tf_op jit(solution)/shard_map/pallas_call | solution.py:337
  28.8 0.8 %slice_bitcast_fusion = (f32[6,8192]{1,0:T(8,128)}, f32[6,8192]{1,0:T(8,128)}) fusion(f32[2,6,8192]{2,1,0:T(8,128)S(1)} %shard_map.50), kind=kLoop, calls=%fused_computation | loop fusion | bytes 786432 | tf_op jit(solution)/shard_map/squeeze | solution.py:371
where the time goes:
time: 29.8 us; the launch traced here: 29.6 us
  Pallas kernels  28.2 us (95%)
  local copies, waits for them, and re-layouts  0.82 us (3%)
  between operations  0.64 us (2%)
    pallas_call x1, Pallas kernels, local(): pl.pallas_call(functools.partial(kernel, n, pixes, group), out_shape=pltp...  28.2 us
    squeeze x1, local copies, waits for them, and re-layouts, local(): return (out[0], out[1])  0.82 us

commit v1 on v0

v1 whole, which is shorter than its diff:
```python
import functools

import jax
import jax.numpy as jnp
from jax import lax
from jax.experimental import pallas as pl
from jax.experimental.pallas import tpu as pltpu
from jax.sharding import PartitionSpec as P

MESH = pl.DeviceIdType.MESH
ridge = 1.0
sentinel = 100.0
lanes = 128
slot = 8


def merge_pairs(lo, hi, r):
    step = r * 2
    if step < hi - lo:
        yield from merge_pairs(lo, hi, step)
        yield from merge_pairs(lo + r, hi, step)
        yield from ((i, i + r) for i in range(lo + r, hi - r, step))
    else:
        yield (lo, lo + r)


def sort_pairs(lo, hi):
    if hi - lo >= 1:
        mid = lo + (hi - lo) // 2
        yield from sort_pairs(lo, mid)
        yield from sort_pairs(mid + 1, hi)
        yield from merge_pairs(lo, hi, 1)


def sort_network(values):
    values = list(values)
    for i, j in sort_pairs(0, len(values) - 1):
        a, b = values[i], values[j]
        values[i], values[j] = jnp.minimum(a, b), jnp.maximum(a, b)
    return values


def kernel(
    n,
    pixes,
    spans,
    x_hbm,
    m_hbm,
    days_ref,
    out_ref,
    x_ref,
    m_ref,
    wide,
    sent,
    got,
    part,
    parts,
    mean_row,
    mean_rows,
    stack,
    mean_tile,
    year_tile,
    flip,
    odd,
    slopes,
    coded,
    load_sem,
    data_send,
    data_recv,
    part_send,
    part_recv,
    mean_send,
    mean_recv,
    code_send,
    code_recv,
    *code,
):
    me = lax.axis_index("date")
    pix = lax.axis_index("pix")
    bands, dates, tile = x_ref.shape
    width = tile // n
    total = n * dates
    starts = [sum(spans[:p]) for p in range(len(spans))]

    def ahead(r):
        return lax.rem(me + r, n)

    def behind(r):
        return lax.rem(me + n - r, n)

    barrier = pltpu.get_barrier_semaphore()

    @pl.loop(1, n)
    def _(r):
        pl.semaphore_signal(barrier, inc=1, device_id={"date": ahead(r)}, device_id_type=MESH)

    for r in range(1, pixes):
        pl.semaphore_signal(barrier, inc=1, device_id={"pix": lax.rem(pix + r, pixes)}, device_id_type=MESH)

    load_x = pltpu.make_async_copy(x_hbm, x_ref, load_sem.at[0])
    load_m = pltpu.make_async_copy(m_hbm, m_ref, load_sem.at[1])
    load_x.start()
    load_m.start()
    stack[...] = jnp.zeros_like(stack)
    coded[...] = jnp.zeros_like(coded)
    load_m.wait()
    load_x.wait()

    def mark(j, carry):
        cols = pl.ds(pl.multiple_of(j * width, lanes), width)
        valid = m_ref[:, cols] > 0
        out = []
        for b in range(bands):
            x = x_ref[b, :, cols].astype(jnp.float32)
            marked = jnp.where(valid, x, sentinel)
            for d in range(dates):
                wide[d * bands + b : d * bands + b + 1, :] = marked[d : d + 1, :]
            out.append(carry[b] + jnp.where(valid, x, 0.0))
        sent[j] = wide[...].astype(jnp.bfloat16)
        out.append(carry[bands] + jnp.where(valid, 1.0, 0.0))
        return tuple(out)

    zero = jnp.zeros((dates, width), jnp.float32)
    sums = lax.fori_loop(0, n, mark, tuple(zero for _ in range(bands + 1)))
    got[me] = sent[me]

    lane = lax.broadcasted_iota(jnp.int32, (dates, lanes), 1)
    date = lax.broadcasted_iota(jnp.int32, (dates, lanes), 0)
    lane_row = lax.broadcasted_iota(jnp.int32, (1, lanes), 1)
    row = jnp.zeros((dates, lanes), jnp.float32)
    for b in range(bands):
        row = row + jnp.where(lane == date * slot + b, jnp.sum(sums[b], axis=1, keepdims=True), 0.0)
    own = (lane >= date * slot) & (lane < (date + 1) * slot)
    count_row = jnp.where(own, jnp.sum(sums[bands], axis=1, keepdims=True), 0.0)
    part[0:1, :] = jnp.sum(row, axis=0, keepdims=True)
    part[1:2, :] = jnp.sum(count_row, axis=0, keepdims=True)
    years = jnp.zeros((1, lanes), jnp.float32)
    for d in range(dates):
        year = jnp.full((1, lanes), days_ref[d], jnp.int32).astype(jnp.float32) / 365.0
        years = jnp.where((lane_row >= d * slot) & (lane_row < (d + 1) * slot), year, years)
    mean_row[1:2, :] = years

    def part_copy(r):
        return pltpu.make_async_remote_copy(
            src_ref=part,
            dst_ref=parts.at[r],
            send_sem=part_send.at[r],
            recv_sem=part_recv.at[r],
            device_id={"pix": lax.rem(pix + r, pixes)},
            device_id_type=MESH,
        )

    def data_copy(r):
        return pltpu.make_async_remote_copy(
            src_ref=sent.at[ahead(r)],
            dst_ref=got.at[me],
            send_sem=data_send.at[r],
            recv_sem=data_recv.at[r],
            device_id={"date": ahead(r)},
            device_id_type=MESH,
        )

    def mean_copy(r):
        return pltpu.make_async_remote_copy(
            src_ref=mean_row,
            dst_ref=mean_rows.at[me],
            send_sem=mean_send.at[r],
            recv_sem=mean_recv.at[r],
            device_id={"date": ahead(r)},
            device_id_type=MESH,
        )

    def code_copy(p, r):
        return pltpu.make_async_remote_copy(
            src_ref=code[p].at[me],
            dst_ref=code[p].at[me],
            send_sem=code_send.at[p, r],
            recv_sem=code_recv.at[p, r],
            device_id={"date": ahead(r)},
            device_id_type=MESH,
        )

    early = min(4, n)
    pl.semaphore_wait(barrier, n - 1 + pixes - 1)
    for r in range(1, pixes):
        part_copy(r).start()

    @pl.loop(1, early)
    def _(r):
        data_copy(r).start()

    csum_row = part[0:1, :]
    cnt_row = part[1:2, :]
    for r in range(1, pixes):
        part_copy(r).wait_recv()
        csum_row = csum_row + parts[r, 0:1, :]
        cnt_row = cnt_row + parts[r, 1:2, :]
    mean_row[0:1, :] = csum_row / jnp.maximum(cnt_row, 1.0)
    mean_rows[me] = mean_row[...]

    @pl.loop(1, n)
    def _(r):
        mean_copy(r).start()

    @pl.loop(early, n)
    def _(r):
        data_copy(r).start()

    @pl.loop(1, n)
    def _(r):
        mean_copy(r).wait_recv()

    for row_index, tile_ref in ((0, mean_tile), (1, year_tile)):
        for j in range(n):
            stack[j : j + 1, :] = mean_rows[j, row_index : row_index + 1, :]
        turned = jnp.transpose(stack[...])
        for j in range(n):
            for d in range(dates):
                column = turned[d * slot : d * slot + bands, j : j + 1]
                tile_ref[j * dates + d] = jnp.broadcast_to(column, (bands, lanes))

    def trend(r, carry):
        j = behind(r)
        fill, s_zero, s_one, s_two, s_y, s_ty = carry
        block = got[j].astype(jnp.float32)
        for d in range(dates):
            x = block[d * bands : (d + 1) * bands, :]
            year = jnp.concatenate([year_tile[j * dates + d]] * (width // lanes), axis=1)
            mean = jnp.concatenate([mean_tile[j * dates + d]] * (width // lanes), axis=1)
            valid = x < 50.0
            y = jnp.where(valid, x - mean, 0.0)
            m = jnp.where(valid, 1.0, 0.0)
            tm = year * m
            s_zero = s_zero + m
            s_one = s_one + tm
            s_two = s_two + year * tm
            s_y = s_y + y
            s_ty = s_ty + year * y
            flip[r * dates + d] = jnp.where(valid, x, fill)
            fill = jnp.where(valid, fill, -fill)
        return (fill, s_zero, s_one, s_two, s_y, s_ty)

    def arrived(r, carry):
        data_copy(r).wait_recv()
        return trend(r, carry)

    half = total // 2
    blank = jnp.zeros((bands, width), jnp.float32)
    sums = trend(0, (blank + sentinel, blank, blank, blank, blank, blank))
    sums = lax.fori_loop(1, n // 2, arrived, sums)

    @pl.loop(0, width // lanes)
    def _(k):
        cols = pl.ds(pl.multiple_of(k * lanes, lanes), lanes)
        for i, value in enumerate(sort_network([flip[i, :, cols] for i in range(half)])):
            flip[i, :, cols] = value

    sums = lax.fori_loop(n // 2, n, arrived, sums)
    fill, s_zero, s_one, s_two, s_y, s_ty = sums
    first = s_zero + ridge
    slopes[...] = (first * s_ty - s_one * s_y) / (first * (s_two + ridge) - s_one * s_one)
    odd[...] = jnp.where(fill < 0.0, 1.0, 0.0)

    def encode(base, values):
        top = jnp.maximum(jnp.max(jnp.abs(values), axis=0, keepdims=True), 1e-30)
        power = jnp.floor(jnp.log2(top))
        whole = jnp.round(values * jnp.exp2(14.0 - power))
        coded[base : base + bands, :] = jnp.clip(whole, -32767.0, 32767.0)
        coded[base + bands : base + bands + 1, :] = power

    def decode(p, j):
        for k in range(spans[p] // lanes):
            values = code[p][j, :, k * lanes : (k + 1) * lanes].astype(jnp.int32).astype(jnp.float32)
            there = pl.ds(pl.multiple_of(j * width + starts[p] + k * lanes, lanes), lanes)
            for o in range(2):
                scale = jnp.exp2(values[o * slot + bands : o * slot + bands + 1, :] - 14.0)
                out_ref[o, :, there] = values[o * slot : o * slot + bands, :] * scale

    for p, span in enumerate(spans):

        @pl.loop(0, span // lanes)
        def _(k):
            cols = pl.ds(pl.multiple_of(starts[p] + k * lanes, lanes), lanes)
            here = pl.ds(pl.multiple_of(k * lanes, lanes), lanes)
            low = [flip[i, :, cols] for i in range(half)]
            high = sort_network([flip[half + i, :, cols] for i in range(half)])
            lower = None
            upper = None
            for i in range(half):
                a, b = low[i], high[half - 1 - i]
                small, large = jnp.minimum(a, b), jnp.maximum(a, b)
                lower = small if lower is None else jnp.maximum(lower, small)
                upper = large if upper is None else jnp.minimum(upper, large)
            median = jnp.where(odd[:, cols] > 0.5, lower, 0.5 * (lower + upper))
            encode(0, median)
            encode(slot, slopes[:, cols])
            code[p][me, :, here] = coded[...].astype(jnp.int32).astype(jnp.int16)

        @pl.loop(1, n)
        def _(r):
            code_copy(p, r).start()

    for p in range(len(spans)):
        decode(p, me)

        @pl.loop(1, n)
        def _(r):
            code_copy(p, r).wait_recv()
            decode(p, behind(r))

    for r in range(1, pixes):
        part_copy(r).wait_send()

    @pl.loop(1, n)
    def _(r):
        mean_copy(r).wait_send()
        data_copy(r).wait_send()
        for p in range(len(spans)):
            code_copy(p, r).wait_send()


def local(n, pixes, reflect, cloud_free, days):
    dates, bands, tile = reflect.shape
    width = tile // n
    spans = [width]
    turned = -(-n // lanes) * lanes
    vmem = pl.BlockSpec(memory_space=pltpu.VMEM)
    hbm = pl.BlockSpec(memory_space=pl.ANY)
    dma = pltpu.SemaphoreType.DMA
    out = pl.pallas_call(
        functools.partial(kernel, n, pixes, spans),
        out_shape=pltpu.VMEM((2, bands, tile), jnp.float32),
        in_specs=[hbm, hbm, pl.BlockSpec(memory_space=pltpu.SMEM)],
        out_specs=vmem,
        scratch_shapes=[
            pltpu.VMEM((bands, dates, tile), jnp.bfloat16),
            pltpu.VMEM((dates, tile), jnp.int32),
            pltpu.VMEM((dates * bands, width), jnp.float32),
            pltpu.VMEM((n, dates * bands, width), jnp.bfloat16),
            pltpu.VMEM((n, dates * bands, width), jnp.bfloat16),
            pltpu.VMEM((2, lanes), jnp.float32),
            pltpu.VMEM((pixes, 2, lanes), jnp.float32),
            pltpu.VMEM((2, lanes), jnp.float32),
            pltpu.VMEM((n, 2, lanes), jnp.float32),
            pltpu.VMEM((turned, lanes), jnp.float32),
            pltpu.VMEM((n * dates, bands, lanes), jnp.float32),
            pltpu.VMEM((n * dates, bands, lanes), jnp.float32),
            pltpu.VMEM((n * dates, bands, width), jnp.float32),
            pltpu.VMEM((bands, width), jnp.float32),
            pltpu.VMEM((bands, width), jnp.float32),
            pltpu.VMEM((2 * slot, lanes), jnp.float32),
            dma((2,)),
            dma((n,)),
            dma((n,)),
            dma((pixes,)),
            dma((pixes,)),
            dma((n,)),
            dma((n,)),
            dma((len(spans), n)),
            dma((len(spans), n)),
            *[pltpu.VMEM((n, 2 * slot, span), jnp.int16) for span in spans],
        ],
        compiler_params=pltpu.CompilerParams(collective_id=0, has_side_effects=True),
    )(jnp.transpose(reflect, (1, 0, 2)), cloud_free, days)
    return (out[0], out[1])


def solution(mesh):
    placed = (P("date", None, "pix"), P("date", "pix"), P("date"))
    return jax.shard_map(
        functools.partial(local, mesh.shape["date"], mesh.shape["pix"]),
        mesh=mesh,
        in_specs=placed,
        out_specs=(P(None, "pix"), P(None, "pix")),
        check_vma=False,
    )
```

time: 29.8 us -> 28.5 us (0.956)
  Pallas kernels: 28.2 us -> 26.9 us
    pallas_call x1, Pallas kernels: 28.2 us -> 26.9 us  [local(): pl.pallas_call(functools.partial(kernel, n, pixes, spans), out_shape=pltp...]
where the time goes in v1:
time: 28.5 us; the launch traced here: 28.3 us
  Pallas kernels  26.9 us (94%)
  local copies, waits for them, and re-layouts  0.82 us (3%)
  between operations  0.64 us (2%)
    pallas_call x1, Pallas kernels, local(): pl.pallas_call(functools.partial(kernel, n, pixes, spans), out_shape=pltp...  26.9 us
    squeeze x1, local copies, waits for them, and re-layouts, local(): return (out[0], out[1])  0.82 us

profile of v1, /device:TPU:0, one launch (start us, length us, event | category | flops | bytes accessed | tf_op | source)
XLA Modules:
  0.0 28.3 jit_solution(16957248203660624295)
XLA Ops:
  0.6 26.9 %shard_map.50 = f32[2,6,8192]{2,1,0:T(8,128)S(1)} custom-call(bf16[6,4,8192]{2,1,0:T(4,128)(2,1)} %bitcast.5, s32[4,8192]{1,0:T(4,128)} %m_hbm.1, s32[4]{0:T(128)} %days_ref.1), custom_call_target="tpu_custom_call" | custom-call | tf_op jit(solution)/shard_map/pallas_call | solution.py:330
  27.5 0.8 %slice_bitcast_fusion = (f32[6,8192]{1,0:T(8,128)}, f32[6,8192]{1,0:T(8,128)}) fusion(f32[2,6,8192]{2,1,0:T(8,128)S(1)} %shard_map.50), kind=kLoop, calls=%fused_computation | loop fusion | bytes 786432 | tf_op jit(solution)/shard_map/squeeze | solution.py:365

commit v2 on v1

--- a/solution.py
+++ b/solution.py
@@ -43,6 +43,7 @@
 def kernel(
     n,
     pixes,
+    group,
     spans,
     x_hbm,
     m_hbm,
@@ -64,6 +65,7 @@
     odd,
     slopes,
     coded,
+    plane_sem,
     load_sem,
     data_send,
     data_recv,
@@ -82,18 +84,23 @@
     total = n * dates
     starts = [sum(spans[:p]) for p in range(len(spans))]
 
+    lines = n // group
+    line = me // group
+    spot = lax.rem(me, group)
+
     def ahead(r):
-        return lax.rem(me + r, n)
+        return lax.rem(line + r // group, lines) * group + lax.rem(spot + lax.rem(r, group), group)
 
     def behind(r):
-        return lax.rem(me + n - r, n)
+        return lax.rem(line + lines - r // group, lines) * group + lax.rem(spot + group - lax.rem(r, group), group)
+
+    stack_line = [a * group for a in range(1, lines)]
+    plane = list(range(1, group))
+    rest = [r for r in range(1, n) if r not in stack_line and r not in plane]
 
     barrier = pltpu.get_barrier_semaphore()
-
-    @pl.loop(1, n)
-    def _(r):
+    for r in stack_line + plane:
         pl.semaphore_signal(barrier, inc=1, device_id={"date": ahead(r)}, device_id_type=MESH)
-
     for r in range(1, pixes):
         pl.semaphore_signal(barrier, inc=1, device_id={"pix": lax.rem(pix + r, pixes)}, device_id_type=MESH)
 
@@ -180,13 +187,12 @@
             device_id_type=MESH,
         )
 
-    early = min(4, n)
-    pl.semaphore_wait(barrier, n - 1 + pixes - 1)
+    pl.semaphore_wait(barrier, len(stack_line) + len(plane) + pixes - 1)
+    for r in plane:
+        pl.semaphore_signal(plane_sem, inc=1, device_id={"date": ahead(r)}, device_id_type=MESH)
     for r in range(1, pixes):
         part_copy(r).start()
-
-    @pl.loop(1, early)
-    def _(r):
+    for r in stack_line + plane:
         data_copy(r).start()
 
     csum_row = part[0:1, :]
@@ -197,13 +203,10 @@
         cnt_row = cnt_row + parts[r, 1:2, :]
     mean_row[0:1, :] = csum_row / jnp.maximum(cnt_row, 1.0)
     mean_rows[me] = mean_row[...]
-
-    @pl.loop(1, n)
-    def _(r):
+    pl.semaphore_wait(plane_sem, len(plane))
+    for r in range(1, n):
         mean_copy(r).start()
-
-    @pl.loop(early, n)
-    def _(r):
+    for r in rest:
         data_copy(r).start()
 
     @pl.loop(1, n)
@@ -323,12 +326,15 @@
     dates, bands, tile = reflect.shape
     width = tile // n
     spans = [width]
+    group = 1
+    while group * group * 4 <= n and n % (group * 2) == 0:
+        group *= 2
     turned = -(-n // lanes) * lanes
     vmem = pl.BlockSpec(memory_space=pltpu.VMEM)
     hbm = pl.BlockSpec(memory_space=pl.ANY)
     dma = pltpu.SemaphoreType.DMA
     out = pl.pallas_call(
-        functools.partial(kernel, n, pixes, spans),
+        functools.partial(kernel, n, pixes, group, spans),
         out_shape=pltpu.VMEM((2, bands, tile), jnp.float32),
         in_specs=[hbm, hbm, pl.BlockSpec(memory_space=pltpu.SMEM)],
         out_specs=vmem,
@@ -349,6 +355,7 @@
             pltpu.VMEM((bands, width), jnp.float32),
             pltpu.VMEM((bands, width), jnp.float32),
             pltpu.VMEM((2 * slot, lanes), jnp.float32),
+            pltpu.SemaphoreType.REGULAR,
             dma((2,)),
             dma((n,)),
             dma((n,)),

time: 28.5 us -> 27.1 us (0.951)
  Pallas kernels: 26.9 us -> 25.5 us
    pallas_call x1, Pallas kernels: 26.9 us -> 25.5 us  [local(): pl.pallas_call(functools.partial(kernel, n, pixes, group, spans), out_sha...]
where the time goes in v2:
time: 27.1 us; the launch traced here: 27 us
  Pallas kernels  25.5 us (94%)
  local copies, waits for them, and re-layouts  0.82 us (3%)
  between operations  0.64 us (2%)
    pallas_call x1, Pallas kernels, local(): pl.pallas_call(functools.partial(kernel, n, pixes, group, spans), out_sha...  25.5 us
    squeeze x1, local copies, waits for them, and re-layouts, local(): return (out[0], out[1])  0.82 us

profile of v2, /device:TPU:0, one launch (start us, length us, event | category | flops | bytes accessed | tf_op | source)
XLA Modules:
  0.0 27.0 jit_solution(17111606850486068361)
XLA Ops:
  0.6 25.5 %shard_map.50 = f32[2,6,8192]{2,1,0:T(8,128)S(1)} custom-call(bf16[6,4,8192]{2,1,0:T(4,128)(2,1)} %bitcast.5, s32[4,8192]{1,0:T(4,128)} %m_hbm.1, s32[4]{0:T(128)} %days_ref.1), custom_call_target="tpu_custom_call" | custom-call | tf_op jit(solution)/shard_map/pallas_call | solution.py:336
  26.2 0.8 %slice_bitcast_fusion = (f32[6,8192]{1,0:T(8,128)}, f32[6,8192]{1,0:T(8,128)}) fusion(f32[2,6,8192]{2,1,0:T(8,128)S(1)} %shard_map.50), kind=kLoop, calls=%fused_computation | loop fusion | bytes 786432 | tf_op jit(solution)/shard_map/squeeze | solution.py:372

commit v3 on v2

--- a/solution.py
+++ b/solution.py
@@ -206,6 +206,10 @@
     pl.semaphore_wait(plane_sem, len(plane))
     for r in range(1, n):
         mean_copy(r).start()
+    @pl.when(lax.rem(pix, 2) == 1)
+    def _():
+        pl.delay(4700)
+
     for r in rest:
         data_copy(r).start()
 

time: 27.1 us -> 25.3 us (0.934)
  the two profiles are of different devices: /device:TPU:0 before, /device:TPU:1 now
where the time goes in v3:
time: 25.3 us; the launch traced here: 25.1 us
  Pallas kernels  23.6 us (93%)
  local copies, waits for them, and re-layouts  0.82 us (3%)
  between operations  0.64 us (3%)
    pallas_call x1, Pallas kernels, local(): pl.pallas_call(functools.partial(kernel, n, pixes, group, spans), out_sha...  23.6 us
    squeeze x1, local copies, waits for them, and re-layouts, local(): return (out[0], out[1])  0.82 us

profile of v3, /device:TPU:1, one launch (start us, length us, event | category | flops | bytes accessed | tf_op | source)
XLA Modules:
  0.0 25.1 jit_solution(4396141855537187364)
XLA Ops:
  0.6 23.6 %shard_map.50 = f32[2,6,8192]{2,1,0:T(8,128)S(1)} custom-call(bf16[6,4,8192]{2,1,0:T(4,128)(2,1)} %bitcast.5, s32[4,8192]{1,0:T(4,128)} %m_hbm.1, s32[4]{0:T(128)} %days_ref.1), custom_call_target="tpu_custom_call" | custom-call | tf_op jit(solution)/shard_map/pallas_call | solution.py:340
  24.3 0.8 %slice_bitcast_fusion = (f32[6,8192]{1,0:T(8,128)}, f32[6,8192]{1,0:T(8,128)}) fusion(f32[2,6,8192]{2,1,0:T(8,128)S(1)} %shard_map.50), kind=kLoop, calls=%fused_computation | loop fusion | bytes 786432 | tf_op jit(solution)/shard_map/squeeze | solution.py:376

commit v4 on v3

--- a/solution.py
+++ b/solution.py
@@ -47,7 +47,7 @@
     spans,
     x_hbm,
     m_hbm,
-    days_ref,
+    days_hbm,
     out_ref,
     x_ref,
     m_ref,
@@ -66,6 +66,7 @@
     slopes,
     coded,
     plane_sem,
+    days_ref,
     load_sem,
     data_send,
     data_recv,
@@ -106,12 +107,15 @@
 
     load_x = pltpu.make_async_copy(x_hbm, x_ref, load_sem.at[0])
     load_m = pltpu.make_async_copy(m_hbm, m_ref, load_sem.at[1])
+    load_days = pltpu.make_async_copy(days_hbm, days_ref, load_sem.at[2])
     load_x.start()
     load_m.start()
+    load_days.start()
     stack[...] = jnp.zeros_like(stack)
     coded[...] = jnp.zeros_like(coded)
     load_m.wait()
     load_x.wait()
+    load_days.wait()
 
     def mark(j, carry):
         cols = pl.ds(pl.multiple_of(j * width, lanes), width)
@@ -303,17 +307,18 @@
             encode(slot, slopes[:, cols])
             code[p][me, :, here] = coded[...].astype(jnp.int32).astype(jnp.int16)
 
-        @pl.loop(1, n)
-        def _(r):
+        for r in range(1, n):
             code_copy(p, r).start()
 
     for p in range(len(spans)):
         decode(p, me)
 
-        @pl.loop(1, n)
-        def _(r):
-            code_copy(p, r).wait_recv()
-            decode(p, behind(r))
+        for r in range(1, n, 3):
+            some = range(r, min(r + 3, n))
+            for q in some:
+                code_copy(p, q).wait_recv()
+            for q in some:
+                decode(p, behind(q))
 
     for r in range(1, pixes):
         part_copy(r).wait_send()
@@ -340,7 +345,7 @@
     out = pl.pallas_call(
         functools.partial(kernel, n, pixes, group, spans),
         out_shape=pltpu.VMEM((2, bands, tile), jnp.float32),
-        in_specs=[hbm, hbm, pl.BlockSpec(memory_space=pltpu.SMEM)],
+        in_specs=[hbm, hbm, hbm],
         out_specs=vmem,
         scratch_shapes=[
             pltpu.VMEM((bands, dates, tile), jnp.bfloat16),
@@ -360,7 +365,8 @@
             pltpu.VMEM((bands, width), jnp.float32),
             pltpu.VMEM((2 * slot, lanes), jnp.float32),
             pltpu.SemaphoreType.REGULAR,
-            dma((2,)),
+            pltpu.SMEM((dates,), jnp.int32),
+            dma((3,)),
             dma((n,)),
             dma((n,)),
             dma((pixes,)),

time: 25.3 us -> 24.4 us (0.964)
  Pallas kernels: 23.6 us -> 22.8 us
    pallas_call x1, Pallas kernels: 23.6 us -> 22.8 us  [local(): pl.pallas_call(functools.partial(kernel, n, pixes, group, spans), out_sha...]
where the time goes in v4:
time: 24.4 us; the launch traced here: 24.2 us
  Pallas kernels  22.8 us (93%)
  local copies, waits for them, and re-layouts  0.82 us (3%)
  between operations  0.64 us (3%)
    pallas_call x1, Pallas kernels, local(): pl.pallas_call(functools.partial(kernel, n, pixes, group, spans), out_sha...  22.8 us
    squeeze x1, local copies, waits for them, and re-layouts, local(): return (out[0], out[1])  0.82 us

profile of v4, /device:TPU:1, one launch (start us, length us, event | category | flops | bytes accessed | tf_op | source)
XLA Modules:
  0.0 24.2 jit_solution(9442866415981503698)
XLA Ops:
  0.6 22.8 %shard_map.50 = f32[2,6,8192]{2,1,0:T(8,128)S(1)} custom-call(bf16[6,4,8192]{2,1,0:T(4,128)(2,1)} %bitcast.5, s32[4,8192]{1,0:T(4,128)} %m_hbm.1, s32[4]{0:T(128)} %days_hbm.1), custom_call_target="tpu_custom_call" | custom-call | tf_op jit(solution)/shard_map/pallas_call | solution.py:345
  23.4 0.8 %slice_bitcast_fusion = (f32[6,8192]{1,0:T(8,128)}, f32[6,8192]{1,0:T(8,128)}) fusion(f32[2,6,8192]{2,1,0:T(8,128)S(1)} %shard_map.50), kind=kLoop, calls=%fused_computation | loop fusion | bytes 786432 | tf_op jit(solution)/shard_map/squeeze | solution.py:382

commit v5 on v4

--- a/solution.py
+++ b/solution.py
@@ -199,23 +199,37 @@
     for r in stack_line + plane:
         data_copy(r).start()
 
-    csum_row = part[0:1, :]
-    cnt_row = part[1:2, :]
-    for r in range(1, pixes):
-        part_copy(r).wait_recv()
-        csum_row = csum_row + parts[r, 0:1, :]
-        cnt_row = cnt_row + parts[r, 1:2, :]
-    mean_row[0:1, :] = csum_row / jnp.maximum(cnt_row, 1.0)
-    mean_rows[me] = mean_row[...]
+    def send_means():
+        csum_row = part[0:1, :]
+        cnt_row = part[1:2, :]
+        for r in range(1, pixes):
+            part_copy(r).wait_recv()
+            csum_row = csum_row + parts[r, 0:1, :]
+            cnt_row = cnt_row + parts[r, 1:2, :]
+        mean_row[0:1, :] = csum_row / jnp.maximum(cnt_row, 1.0)
+        mean_rows[me] = mean_row[...]
+        for r in range(1, n):
+            mean_copy(r).start()
+
+    def send_rest():
+        for r in rest:
+            data_copy(r).start()
+
     pl.semaphore_wait(plane_sem, len(plane))
-    for r in range(1, n):
-        mean_copy(r).start()
+
+    @pl.when(lax.rem(pix, 2) == 0)
+    def _():
+        for r in rest[: len(rest) // 3]:
+            data_copy(r).start()
+        send_means()
+        for r in rest[len(rest) // 3 :]:
+            data_copy(r).start()
+
     @pl.when(lax.rem(pix, 2) == 1)
     def _():
+        send_means()
         pl.delay(4700)
-
-    for r in rest:
-        data_copy(r).start()
+        send_rest()
 
     @pl.loop(1, n)
     def _(r):
@@ -303,10 +317,11 @@
                 lower = small if lower is None else jnp.maximum(lower, small)
                 upper = large if upper is None else jnp.minimum(upper, large)
             median = jnp.where(odd[:, cols] > 0.5, lower, 0.5 * (lower + upper))
-            encode(0, median)
-            encode(slot, slopes[:, cols])
-            code[p][me, :, here] = coded[...].astype(jnp.int32).astype(jnp.int16)
-
+            odd[:, cols] = median
+
+        encode(0, odd[...])
+        encode(slot, slopes[...])
+        code[p][me] = coded[...].astype(jnp.int32).astype(jnp.int16)
         for r in range(1, n):
             code_copy(p, r).start()
 
@@ -363,7 +378,7 @@
             pltpu.VMEM((n * dates, bands, width), jnp.float32),
             pltpu.VMEM((bands, width), jnp.float32),
             pltpu.VMEM((bands, width), jnp.float32),
-            pltpu.VMEM((2 * slot, lanes), jnp.float32),
+            pltpu.VMEM((2 * slot, width), jnp.float32),
             pltpu.SemaphoreType.REGULAR,
             pltpu.SMEM((dates,), jnp.int32),
             dma((3,)),

time: 24.4 us -> 24.3 us (level)
  no operation moved by 1% of the time
where the time goes in v5:
time: 24.3 us; the launch traced here: 24.1 us
  Pallas kernels  22.6 us (93%)
  local copies, waits for them, and re-layouts  0.82 us (3%)
  between operations  0.64 us (3%)
    pallas_call x1, Pallas kernels, local(): pl.pallas_call(functools.partial(kernel, n, pixes, group, spans), out_sha...  22.6 us
    squeeze x1, local copies, waits for them, and re-layouts, local(): return (out[0], out[1])  0.82 us

profile of v5, /device:TPU:1, one launch (start us, length us, event | category | flops | bytes accessed | tf_op | source)
XLA Modules:
  0.0 24.1 jit_solution(6055881507306357313)
XLA Ops:
  0.6 22.6 %shard_map.50 = f32[2,6,8192]{2,1,0:T(8,128)S(1)} custom-call(bf16[6,4,8192]{2,1,0:T(4,128)(2,1)} %bitcast.5, s32[4,8192]{1,0:T(4,128)} %m_hbm.1, s32[4]{0:T(128)} %days_hbm.1), custom_call_target="tpu_custom_call" | custom-call | tf_op jit(solution)/shard_map/pallas_call | solution.py:360
  23.3 0.8 %slice_bitcast_fusion = (f32[6,8192]{1,0:T(8,128)}, f32[6,8192]{1,0:T(8,128)}) fusion(f32[2,6,8192]{2,1,0:T(8,128)S(1)} %shard_map.50), kind=kLoop, calls=%fused_computation | loop fusion | bytes 786432 | tf_op jit(solution)/shard_map/squeeze | solution.py:397

commit v6 on v5

--- a/solution.py
+++ b/solution.py
@@ -328,8 +328,8 @@
     for p in range(len(spans)):
         decode(p, me)
 
-        for r in range(1, n, 3):
-            some = range(r, min(r + 3, n))
+        for r in range(1, n, 5):
+            some = range(r, min(r + 5, n))
             for q in some:
                 code_copy(p, q).wait_recv()
             for q in some:

time: 24.3 us -> 24.3 us (level)
  no operation moved by 1% of the time
where the time goes in v6:
time: 24.3 us; the launch traced here: 24.1 us
  Pallas kernels  22.7 us (93%)
  local copies, waits for them, and re-layouts  0.82 us (3%)
  between operations  0.64 us (3%)
    pallas_call x1, Pallas kernels, local(): pl.pallas_call(functools.partial(kernel, n, pixes, group, spans), out_sha...  22.7 us
    squeeze x1, local copies, waits for them, and re-layouts, local(): return (out[0], out[1])  0.82 us

profile of v6, /device:TPU:1, one launch (start us, length us, event | category | flops | bytes accessed | tf_op | source)
XLA Modules:
  0.0 24.1 jit_solution(11003180104380290214)
XLA Ops:
  0.6 22.7 %shard_map.50 = f32[2,6,8192]{2,1,0:T(8,128)S(1)} custom-call(bf16[6,4,8192]{2,1,0:T(4,128)(2,1)} %bitcast.5, s32[4,8192]{1,0:T(4,128)} %m_hbm.1, s32[4]{0:T(128)} %days_hbm.1), custom_call_target="tpu_custom_call" | custom-call | tf_op jit(solution)/shard_map/pallas_call | solution.py:360
  23.3 0.8 %slice_bitcast_fusion = (f32[6,8192]{1,0:T(8,128)}, f32[6,8192]{1,0:T(8,128)}) fusion(f32[2,6,8192]{2,1,0:T(8,128)S(1)} %shard_map.50), kind=kLoop, calls=%fused_computation | loop fusion | bytes 786432 | tf_op jit(solution)/shard_map/squeeze | solution.py:397
